TPU v7x, 32 devices: a whole 2x2x4 slice. The times are simulated.
32 devices in a mesh: grid: 2 (over x), prow: 4 (over y, core), pcol: 4 (over z).
Axes of the slice: x: 2, y: 2, z: 4, core: 2. Of those that a mesh axis runs over, the one named last changes fastest.
Arguments:
- sub_rhs: float32 [2, 3, 64, 3072], P('grid', None, None, 'prow'), may hold values from -6 to 6
- root_rhs: float32 [64, 3072], P(None, 'prow'), may hold values from -6 to 6
- diag_inverse: bfloat16 [3, 3072, 6144], P(None, 'prow', ('grid', 'pcol'))
- root_inverse: bfloat16 [3072, 3072], P('prow', 'grid')
- inner_factor: bfloat16 [3, 6144, 3072], P(None, ('grid', 'pcol'), 'prow'), may hold values from -0.078125 to 0.078125
- inner_mask: int32 [3, 48, 24], P(None, ('grid', 'pcol')), may hold values 0 or 1
- root_factor: bfloat16 [3, 6144, 3072], P(None, ('grid', 'pcol'), 'prow'), may hold values from -0.078125 to 0.078125
- root_mask: int32 [3, 48, 24], P(None, ('grid', 'pcol')), may hold values 0 or 1
Outputs:
- sub_solution: float32 [3, 64, 6144], P(None, None, ('grid', 'pcol'))
- root_solution: float32 [64, 3072], P(None, 'grid')
Inputs may be any that keep to these rules, and one draw needn't show every extreme that they name: `inner_mask`: 1 keeps a tile of 128 x 128 entries, 0 makes it zero. `root_mask`: 1 keeps a tile of 128 x 128 entries, 0 makes it zero.
All inputs are finite; a program needn't handle non-finite values. No bound on the sum of `inner_mask` or of `root_mask` on one device may be relied on, other than what follows from the above.
Results may differ from a plain program's by a relative error of at most 0.0065.
Values sent between devices are 32-bit elements; how exact they have to be, the bound alone decides.
A program may use at most 64 MiB of HBM per device.

v0:
```python
import jax
import jax.numpy as jnp
from jax import lax
from jax.sharding import PartitionSpec as P

NS = 3072
LEVELS = 3
TILE = 128


def from_partner(shard, axis, bit):
    return lax.ppermute(shard, axis, [(i, i ^ 1 << bit) for i in range(lax.axis_size(axis))])


def selector(positions, count):
    return (positions[:, None] // TILE == jnp.arange(count)[None, :]).astype(jnp.float32)


def masked(factor, mask, row_select, col_select):
    expanded = jnp.dot(jnp.dot(row_select, mask.astype(jnp.float32)), col_select.T)
    return factor * expanded.astype(jnp.bfloat16)


def solve_block(residual, inverse):
    partial_sum = jnp.dot(
        residual.astype(jnp.bfloat16), inverse, preferred_element_type=jnp.float32
    )
    return lax.psum(partial_sum, "prow")


def group_sum(partial_sum, owners):
    summed = partial_sum
    for bit_number in range(owners.bit_length() - 1):
        summed = summed + from_partner(summed, "pcol", bit_number)
    return summed


def shards(
    sub_rhs, root_rhs, diag_inverse, root_inverse, inner_factor, inner_mask, root_factor, root_mask
):
    rows_here = inner_factor.shape[1]
    out_cols = inner_factor.shape[2]
    owners = NS // rows_here
    own_tree = lax.axis_index("pcol") // owners
    col_positions = lax.axis_index("prow") * out_cols + jnp.arange(out_cols)
    row_select = selector(jnp.arange(rows_here), inner_mask.shape[1])
    col_select = selector(col_positions, inner_mask.shape[2])
    own_rhs = lax.dynamic_index_in_dim(sub_rhs, own_tree, 0, keepdims=False)
    kept = []
    solved_all = []
    pair = 0
    for level in range(LEVELS):
        residual = own_rhs[level]
        if level > 0:
            local_update = jnp.zeros(residual.shape, jnp.float32)
            for source in range(level):
                factor_tile = masked(inner_factor[pair], inner_mask[pair], row_select, col_select)
                local_update = local_update + jnp.dot(
                    kept[source], factor_tile, preferred_element_type=jnp.float32
                )
                pair += 1
            residual = residual - group_sum(local_update, owners)
        solved = solve_block(residual, diag_inverse[level])
        solved_all.append(solved)
        kept.append(solved.astype(jnp.bfloat16))
    root_local = jnp.zeros(root_rhs.shape, jnp.float32)
    for source in range(LEVELS):
        factor_tile = masked(root_factor[source], root_mask[source], row_select, col_select)
        root_local = root_local + jnp.dot(
            kept[source], factor_tile, preferred_element_type=jnp.float32
        )
    across = lax.psum(root_local, "pcol")
    root_update = lax.psum(across, "grid")
    root_solution = solve_block(root_rhs - root_update, root_inverse)
    return (jnp.stack(solved_all), root_solution)


def solution(mesh):
    return jax.shard_map(
        shards,
        mesh=mesh,
        in_specs=(
            P("grid", None, None, "prow"),
            P(None, "prow"),
            P(None, "prow", ("grid", "pcol")),
            P("prow", "grid"),
            P(None, ("grid", "pcol"), "prow"),
            P(None, ("grid", "pcol"), None),
            P(None, ("grid", "pcol"), "prow"),
            P(None, ("grid", "pcol"), None),
        ),
        out_specs=(P(None, None, ("grid", "pcol")), P(None, "grid")),
        check_vma=False,
    )
```

profile of v0, /device:TPU:0, one launch (start us, length us, event | category | flops | bytes accessed | tf_op | source)
XLA Modules:
  0.0 262.5 jit_solution(7148002226130458398)
XLA Ops:
  7.2 2.5 fusion.22
  11.0 34.6 %all-reduce.7.cloned.1.call-done = f32[64,768]{1,0:T(8,128)} async-done(((f32[64,768]{1,0:T(8,128)}), f32[64,768]{1,0:T(8,128)}) %all-reduce.7.cloned.1.call-update) | async-done | bytes 196624 | tf_op jit(solution)/shard_map/psum | solution.py:28
  45.7 2.1 fusion.11
  50.3 3.2 %collective-permute-done = f32[64,768]{1,0:T(8,128)S(1)} collective-permute-done((f32[64,768]{1,0:T(8,128)S(1)}, f32[64,768]{1,0:T(8,128)S(1)}, u32[]{:S(2)}, u32[]{:S(2)}) %collective-permute-start) | collective-permute-done | bytes 196640 | tf_op jit(solution)/shard_map/ppermute | solution.py:12
  53.6 2.5 collective-permute-start.1
  56.0 1.7 fusion.37
  57.7 5.2 %collective-permute-done.1 = f32[64,768]{1,0:T(8,128)S(1)} collective-permute-done((f32[64,768]{1,0:T(8,128)S(1)}, f32[64,768]{1,0:T(8,128)S(1)}, u32[]{:S(2)}, u32[]{:S(2)}) %collective-permute-start.1) | collective-permute-done | bytes 196640 | tf_op jit(solution)/shard_map/ppermute | solution.py:12
  62.9 2.3 fusion.19
  66.3 32.6 %all-reduce.9.cloned.1.call-done = f32[64,768]{1,0:T(8,128)} async-done(((f32[64,768]{1,0:T(8,128)}), f32[64,768]{1,0:T(8,128)}) %all-reduce.9.cloned.1.call-update) | async-done | bytes 196624 | tf_op jit(solution)/shard_map/psum | solution.py:28
  98.8 2.8 %fusion.9 = f32[64,768]{1,0:T(8,128)} fusion(bf16[768,24]{1,0:T(8,128)(2,1)S(1)} %fusion.39, bf16[3,768,768]{2,1,0:T(8,128)(2,1)} %param.12, s32[768]{0:T(1024)S(1)} %copy-done.10, f32[64,768]{1,0:T(8,128)} %all-reduce.9.cloned.1.call-done), kind=kOutput, calls=%fused_computation.15 | convolution fusion | flops 104466432 | bytes 1612800 | tf_op jit(solution)/shard_map/dot_general | solution.py:58
  101.7 2.2 fusion.33
  106.4 3.2 %collective-permute-done.2 = f32[64,768]{1,0:T(8,128)S(1)} collective-permute-done((f32[64,768]{1,0:T(8,128)S(1)}, f32[64,768]{1,0:T(8,128)S(1)}, u32[]{:S(2)}, u32[]{:S(2)}) %collective-permute-start.2) | collective-permute-done | bytes 196640 | tf_op jit(solution)/shard_map/ppermute | solution.py:12
  110.6 2.5 collective-permute-start.3
  113.0 2.8 %fusion.7 = f32[64,768]{1,0:T(8,128)} fusion(bf16[768,24]{1,0:T(8,128)(2,1)} %fusion.37, bf16[3,768,768]{2,1,0:T(8,128)(2,1)} %param.14, s32[768]{0:T(1024)} %add_select_fusion, f32[64,768]{1,0:T(8,128)S(1)} %copy-done.4), kind=kOutput, calls=%fused_computation.13 | convolution fusion | flops 104466432 | bytes 1773568 | tf_op jit(solution)/shard_map/dot_general | solution.py:69
  115.9 4.1 %collective-permute-done.3 = f32[64,768]{1,0:T(8,128)} collective-permute-done((f32[64,768]{1,0:T(8,128)S(1)}, f32[64,768]{1,0:T(8,128)}, u32[]{:S(2)}, u32[]{:S(2)}) %collective-permute-start.3) | collective-permute-done | bytes 196640 | tf_op jit(solution)/shard_map/ppermute | solution.py:12
  120.0 2.4 fusion.15
  122.5 2.1 fusion.34
  124.6 31.4 %all-reduce.11.cloned.1.call-done = f32[64,768]{1,0:T(8,128)} async-done(((f32[64,768]{1,0:T(8,128)}), f32[64,768]{1,0:T(8,128)}) %all-reduce.11.cloned.1.call-update) | async-done | bytes 196624 | tf_op jit(solution)/shard_map/psum | solution.py:28
  156.0 2.8 %fusion.35 = f32[64,768]{1,0:T(8,128)} fusion(f32[64,768]{1,0:T(8,128)S(1)} %fusion.34, bf16[768,24]{1,0:T(8,128)(2,1)S(1)} %copy-done.6, bf16[3,768,768]{2,1,0:T(8,128)(2,1)} %param.14, s32[768]{0:T(1024)S(1)} %copy-done.11, f32[64,768]{1,0:T(8,128)} %all-reduce.11.cloned.1.call-done), kind=kOutput, calls=%fused_computation.41 | convolution fusion | flops 104515584 | bytes 1809408 | tf_op jit(solution)/shard_map/dot_general | solution.py:69
  158.9 35.1 %all-reduce.13.cloned.1.call-done = f32[64,768]{1,0:T(8,128)} async-done(((f32[64,768]{1,0:T(8,128)}), f32[64,768]{1,0:T(8,128)}) %all-reduce.13.cloned.1.call-update) | async-done | bytes 196624 | tf_op jit(solution)/shard_map/psum | solution.py:72
  194.1 24.1 %all-reduce.15.cloned.1.call-done = f32[64,768]{1,0:T(8,128)} async-done(((f32[64,768]{1,0:T(8,128)}), f32[64,768]{1,0:T(8,128)}) %all-reduce.15.cloned.1.call-update) | async-done | bytes 196624 | tf_op jit(solution)/shard_map/psum | solution.py:73
  218.3 2.2 fusion.62
  221.4 32.5 %all-reduce.17.cloned.1.call-done = f32[64,1536]{1,0:T(8,128)} async-done(((f32[64,1536]{1,0:T(8,128)}), f32[64,1536]{1,0:T(8,128)}) %all-reduce.17.cloned.1.call-update) | async-done | bytes 393232 | tf_op jit(solution)/shard_map/psum | solution.py:28
  253.9 1.8 copy.16
  (48 shorter events, 9.4 us)
Async XLA Ops:
  7.2 211.1 %copy-start = (bf16[768,1536]{1,0:T(8,128)(2,1)S(1)}, bf16[768,1536]{1,0:T(8,128)(2,1)}, u32[]{:S(2)}) copy-start(bf16[768,1536]{1,0:T(8,128)(2,1)} %param.11) | copy-start | bytes 7077892
  7.2 2.7 %copy-start.8 = (s32[3,6,24]{2,1,0:T(8,128)S(1)}, s32[3,6,24]{2,1,0:T(8,128)}, u32[]{:S(2)}) copy-start(s32[3,6,24]{2,1,0:T(8,128)} %param.13) | copy-start | bytes 5188
  7.2 38.5 %all-reduce.7.cloned.1.call-start = ((), (), s32[]{:S(2)}) async-start(), calls=%async_computation | async-start | bytes 393216 | tf_op jit(solution)/shard_map/psum | solution.py:28
  9.8 89.0 %all-reduce.9.cloned.1.call-start = ((), (), s32[]{:S(2)}) async-start(), calls=%async_computation.1 | async-start | bytes 393216 | tf_op jit(solution)/shard_map/psum | solution.py:28
  11.0 51.9 %copy-start.1 = (f32[1,3,64,768]{3,2,1,0:T(8,128)S(1)}, f32[1,3,64,768]{3,2,1,0:T(8,128)}, u32[]{:S(2)}) copy-start(f32[1,3,64,768]{3,2,1,0:T(8,128)} %param.8) | copy-start | bytes 1769476
  47.8 5.7 %collective-permute-start = (f32[64,768]{1,0:T(8,128)S(1)}, f32[64,768]{1,0:T(8,128)S(1)}, u32[]{:S(2)}, u32[]{:S(2)}) collective-permute-start(f32[64,768]{1,0:T(8,128)S(1)} %fusion.11), channel_id=1, source_target_pairs={{0,1},{1,0},{2,3},{3,2},{4,5},{5,4},{6,7},{7,6},{8,9},{9,8},{10,11... | collective-permute-start | bytes 589832 | tf_op jit(solution)/shard_map/ppermute | solution.py:12
  53.6 11.7 %copy-start.9 = (s32[3,6,24]{2,1,0:T(8,128)S(1)}, s32[3,6,24]{2,1,0:T(8,128)}, u32[]{:S(2)}) copy-start(s32[3,6,24]{2,1,0:T(8,128)} %param.15) | copy-start | bytes 5188
  53.6 9.4 %collective-permute-start.1 = (f32[64,768]{1,0:T(8,128)S(1)}, f32[64,768]{1,0:T(8,128)S(1)}, u32[]{:S(2)}, u32[]{:S(2)}) collective-permute-start(f32[64,768]{1,0:T(8,128)S(1)} %add.60), channel_id=1, source_target_pairs={{0,2},{1,3},{2,0},{3,1},{4,6},{5,7},{6,4},{7,5},{8,10},{9,11},{10,... | collective-permute-start | bytes 589832 | tf_op jit(solution)/shard_map/ppermute | solution.py:12
  57.7 41.1 %copy-start.10 = (s32[768]{0:T(1024)S(1)}, s32[768]{0:T(1024)}, u32[]{:S(2)}) copy-start(s32[768]{0:T(1024)} %add_select_fusion) | copy-start | bytes 9220
  65.2 36.4 %copy-start.3 = (f32[64,768]{1,0:T(8,128)S(1)}, f32[64,768]{1,0:T(8,128)}, u32[]{:S(2)}) copy-start(f32[64,768]{1,0:T(8,128)} %all-reduce.7.cloned.1.call-done) | copy-start | bytes 589828
  65.2 90.8 %all-reduce.11.cloned.1.call-start = ((), (), s32[]{:S(2)}) async-start(), calls=%async_computation.2 | async-start | bytes 393216 | tf_op jit(solution)/shard_map/psum | solution.py:28
  101.7 11.4 %copy-start.4 = (f32[64,768]{1,0:T(8,128)S(1)}, f32[64,768]{1,0:T(8,128)}, u32[]{:S(2)}) copy-start(f32[64,768]{1,0:T(8,128)} %all-reduce.9.cloned.1.call-done) | copy-start | bytes 589828
  103.9 2.5 copy-start.7
  103.9 5.7 %collective-permute-start.2 = (f32[64,768]{1,0:T(8,128)S(1)}, f32[64,768]{1,0:T(8,128)S(1)}, u32[]{:S(2)}, u32[]{:S(2)}) collective-permute-start(f32[64,768]{1,0:T(8,128)S(1)} %fusion.33), channel_id=1, source_target_pairs={{0,1},{1,0},{2,3},{3,2},{4,5},{5,4},{6,7},{7,6},{8,9},{9,8},{10,11... | collective-permute-start | bytes 589832 | tf_op jit(solution)/shard_map/ppermute | solution.py:12
  110.6 9.5 %collective-permute-start.3 = (f32[64,768]{1,0:T(8,128)S(1)}, f32[64,768]{1,0:T(8,128)}, u32[]{:S(2)}, u32[]{:S(2)}) collective-permute-start(f32[64,768]{1,0:T(8,128)S(1)} %add.63), channel_id=1, source_target_pairs={{0,2},{1,3},{2,0},{3,1},{4,6},{5,7},{6,4},{7,5},{8,10},{9,11},{10,... | collective-permute-start | bytes 589832 | tf_op jit(solution)/shard_map/ppermute | solution.py:12
  115.9 6.6 %copy-start.11 = (s32[768]{0:T(1024)S(1)}, s32[768]{0:T(1024)}, u32[]{:S(2)}) copy-start(s32[768]{0:T(1024)} %add_select_fusion) | copy-start | bytes 9220
  122.4 33.6 %copy-start.6 = (bf16[768,24]{1,0:T(8,128)(2,1)S(1)}, bf16[768,24]{1,0:T(8,128)(2,1)}, u32[]{:S(2)}) copy-start(bf16[768,24]{1,0:T(8,128)(2,1)} %fusion.36) | copy-start | bytes 110596
  122.4 71.6 %all-reduce.13.cloned.1.call-start = ((), (), s32[]{:S(2)}) async-start(), calls=%async_computation.3 | async-start | bytes 393216 | tf_op jit(solution)/shard_map/psum | solution.py:72
  124.6 93.6 %copy-start.2 = (f32[64,768]{1,0:T(8,128)S(1)}, f32[64,768]{1,0:T(8,128)}, u32[]{:S(2)}) copy-start(f32[64,768]{1,0:T(8,128)} %param.9) | copy-start | bytes 589828
  158.9 59.4 %all-reduce.15.cloned.1.call-start = ((), (), s32[]{:S(2)}) async-start(), calls=%async_computation.4 | async-start | bytes 393216 | tf_op jit(solution)/shard_map/psum | solution.py:73
  194.1 26.4 %copy-start.5 = (f32[64,768]{1,0:T(8,128)S(1)}, f32[64,768]{1,0:T(8,128)}, u32[]{:S(2)}) copy-start(f32[64,768]{1,0:T(8,128)} %all-reduce.11.cloned.1.call-done) | copy-start | bytes 589828
  194.1 59.8 %all-reduce.17.cloned.1.call-start = ((), (), s32[]{:S(2)}) async-start(), calls=%async_computation.5 | async-start | bytes 786432 | tf_op jit(solution)/shard_map/psum | solution.py:28
Sparse Core Ops, SparseCore 0:
  10.9 34.7 all-reduce.6
  65.3 33.4 all-reduce.8
  122.6 33.4 all-reduce.10
  159.0 34.9 all-reduce.12
  196.2 22.0 all-reduce.14
  221.1 32.7 all-reduce.16
where the time goes:
time: 263 us
  waiting for transfers between devices  206 us (78%)
  matrix products  29.5 us (11%)
  between operations  14.3 us (5%)
  starting transfers between devices  8.29 us (3%)
    psum x4, waiting for transfers between devices, solve_block(): return lax.psum(partial_sum, 'prow')  131 us
    psum x1, waiting for transfers between devices, shards(): across = lax.psum(root_local, 'pcol')  35.1 us
    psum x1, waiting for transfers between devices, shards(): root_update = lax.psum(across, 'grid')  24.1 us
    ppermute x4, waiting for transfers between devices, from_partner(): lax.ppermute(shard, axis, [(i, i ^ 1 << bit) for i in range(lax.axis_size...  15.8 us
    dot_general x6, matrix products, shards(): jnp.dot(kept[source], factor_tile, preferred_element_type=jnp.float32)  14.9 us
    dot_general x4, matrix products, solve_block(): jnp.dot(residual.astype(jnp.bfloat16), inverse, preferred_element_type=jn...  9.38 us
    ppermute x4, starting transfers between devices, from_partner(): lax.ppermute(shard, axis, [(i, i ^ 1 << bit) for i in range(lax.axis_size...  8.05 us
  transfers between devices with their start and end apart: 10, of which 10 were waited for; matrix products, arithmetic and copies ran while one was open for 4% of the time, Pallas kernels for 0%

commit v1 on v0

--- a/solution.py
+++ b/solution.py
@@ -6,6 +6,16 @@
 NS = 3072
 LEVELS = 3
 TILE = 128
+
+
+def matrix_find(inner_x):
+    p_count = jax.lax.psum(1, "pcol")
+    latest = inner_x
+    for pp in [hop_no for hop_no in (1, 2, 4, 8, 16) if hop_no < p_count]:
+        latest = latest + jax.lax.ppermute(
+            latest, "pcol", tuple(((m, m ^ pp) for m in range(p_count)))
+        )
+    return latest
 
 
 def from_partner(shard, axis, bit):
@@ -69,7 +79,7 @@
         root_local = root_local + jnp.dot(
             kept[source], factor_tile, preferred_element_type=jnp.float32
         )
-    across = lax.psum(root_local, "pcol")
+    across = matrix_find(root_local)
     root_update = lax.psum(across, "grid")
     root_solution = solve_block(root_rhs - root_update, root_inverse)
     return (jnp.stack(solved_all), root_solution)

time: 263 us -> 242 us (0.920)
  waiting for transfers between devices: 206 us -> 182 us
  starting transfers between devices: 8.29 us -> 12.3 us
    psum x1 -> x0, waiting for transfers between devices: 35.1 us -> none  [shards(): across = lax.psum(root_local, 'pcol')]
    ppermute x0 -> x2, waiting for transfers between devices: none -> 11.1 us  [matrix_find(): jax.lax.ppermute(latest, 'pcol', tuple(((m, m ^ pp) for m in range(p_coun...]
    ppermute x0 -> x2, starting transfers between devices: none -> 4.02 us  [matrix_find(): jax.lax.ppermute(latest, 'pcol', tuple(((m, m ^ pp) for m in range(p_coun...]
  transfers between devices with their start and end apart: 10 -> 11, of which waited for: 10 -> 11; matrix products, arithmetic and copies ran while one was open for 4% -> 5% of each run, Pallas kernels for 0% -> 0%
where the time goes in v1:
time: 242 us
  waiting for transfers between devices  182 us (75%)
  matrix products  28.8 us (12%)
  between operations  13.9 us (6%)
  starting transfers between devices  12.3 us (5%)
  other arithmetic  3.17 us (1%)
    psum x4, waiting for transfers between devices, solve_block(): return lax.psum(partial_sum, 'prow')  131 us
    psum x1, waiting for transfers between devices, shards(): root_update = lax.psum(across, 'grid')  24 us
    ppermute x4, waiting for transfers between devices, from_partner(): lax.ppermute(shard, axis, [(i, i ^ 1 << bit) for i in range(lax.axis_size...  15.8 us
    dot_general x6, matrix products, shards(): jnp.dot(kept[source], factor_tile, preferred_element_type=jnp.float32)  14.3 us
    ppermute x2, waiting for transfers between devices, matrix_find(): jax.lax.ppermute(latest, 'pcol', tuple(((m, m ^ pp) for m in range(p_coun...  11.1 us
    dot_general x4, matrix products, solve_block(): jnp.dot(residual.astype(jnp.bfloat16), inverse, preferred_element_type=jn...  9.38 us
    ppermute x4, starting transfers between devices, from_partner(): lax.ppermute(shard, axis, [(i, i ^ 1 << bit) for i in range(lax.axis_size...  8.05 us
    dot_general x6, matrix products, masked(): jnp.dot(row_select, mask.astype(jnp.float32))  5.14 us
  transfers between devices with their start and end apart: 11, of which 11 were waited for; matrix products, arithmetic and copies ran while one was open for 5% of the time, Pallas kernels for 0%

profile of v1, /device:TPU:0, one launch (start us, length us, event | category | flops | bytes accessed | tf_op | source)
XLA Modules:
  0.0 242.0 jit_solution(14567248684123717870)
XLA Ops:
  7.2 2.5 %fusion.22 = f32[64,768]{1,0:T(8,128)} fusion(bf16[3,768,768]{2,1,0:T(8,128)(2,1)} %param.10, f32[1,3,64,768]{3,2,1,0:T(8,128)} %param.8), kind=kOutput, calls=%fused_computation.28 | convolution fusion | flops 75497472 | bytes 1474560 | tf_op jit(solution)/shard_map/dot_general | solution.py:35
  11.1 34.6 %all-reduce.6.cloned.1.call-done = f32[64,768]{1,0:T(8,128)} async-done(((f32[64,768]{1,0:T(8,128)}), f32[64,768]{1,0:T(8,128)}) %all-reduce.6.cloned.1.call-update) | async-done | bytes 196624 | tf_op jit(solution)/shard_map/psum | solution.py:38
  45.7 2.1 fusion.11
  50.3 3.2 %collective-permute-done = f32[64,768]{1,0:T(8,128)S(1)} collective-permute-done((f32[64,768]{1,0:T(8,128)S(1)}, f32[64,768]{1,0:T(8,128)S(1)}, u32[]{:S(2)}, u32[]{:S(2)}) %collective-permute-start) | collective-permute-done | bytes 196640 | tf_op jit(solution)/shard_map/ppermute | solution.py:22
  53.6 2.5 %collective-permute-start.1 = (f32[64,768]{1,0:T(8,128)S(1)}, f32[64,768]{1,0:T(8,128)S(1)}, u32[]{:S(2)}, u32[]{:S(2)}) collective-permute-start(f32[64,768]{1,0:T(8,128)S(1)} %add.64), channel_id=1, source_target_pairs={{0,2},{1,3},{2,0},{3,1},{4,6},{5,7},{6,4},{7,5},{8,10},{9,11},{10,... | collective-permute-start | bytes 589832 | tf_op jit(solution)/shard_map/ppermute | solution.py:22
  57.7 5.2 %collective-permute-done.1 = f32[64,768]{1,0:T(8,128)S(1)} collective-permute-done((f32[64,768]{1,0:T(8,128)S(1)}, f32[64,768]{1,0:T(8,128)S(1)}, u32[]{:S(2)}, u32[]{:S(2)}) %collective-permute-start.1) | collective-permute-done | bytes 196640 | tf_op jit(solution)/shard_map/ppermute | solution.py:22
  62.9 2.3 fusion.19
  66.3 32.6 %all-reduce.8.cloned.1.call-done = f32[64,768]{1,0:T(8,128)} async-done(((f32[64,768]{1,0:T(8,128)}), f32[64,768]{1,0:T(8,128)}) %all-reduce.8.cloned.1.call-update) | async-done | bytes 196624 | tf_op jit(solution)/shard_map/psum | solution.py:38
  98.8 2.8 %fusion.9 = f32[64,768]{1,0:T(8,128)} fusion(bf16[768,24]{1,0:T(8,128)(2,1)S(1)} %fusion.39, bf16[3,768,768]{2,1,0:T(8,128)(2,1)} %param.12, s32[768]{0:T(1024)S(1)} %copy-done.10, f32[64,768]{1,0:T(8,128)} %all-reduce.8.cloned.1.call-done), kind=kOutput, calls=%fused_computation.15 | convolution fusion | flops 104466432 | bytes 1612800 | tf_op jit(solution)/shard_map/dot_general | solution.py:68
  101.7 2.2 fusion.33
  106.4 3.2 %collective-permute-done.2 = f32[64,768]{1,0:T(8,128)S(1)} collective-permute-done((f32[64,768]{1,0:T(8,128)S(1)}, f32[64,768]{1,0:T(8,128)S(1)}, u32[]{:S(2)}, u32[]{:S(2)}) %collective-permute-start.2) | collective-permute-done | bytes 196640 | tf_op jit(solution)/shard_map/ppermute | solution.py:22
  110.6 2.5 %collective-permute-start.3 = (f32[64,768]{1,0:T(8,128)S(1)}, f32[64,768]{1,0:T(8,128)}, u32[]{:S(2)}, u32[]{:S(2)}) collective-permute-start(f32[64,768]{1,0:T(8,128)S(1)} %add.67), channel_id=1, source_target_pairs={{0,2},{1,3},{2,0},{3,1},{4,6},{5,7},{6,4},{7,5},{8,10},{9,11},{10,... | collective-permute-start | bytes 589832 | tf_op jit(solution)/shard_map/ppermute | solution.py:22
  113.0 2.8 %fusion.7 = f32[64,768]{1,0:T(8,128)} fusion(bf16[768,24]{1,0:T(8,128)(2,1)} %fusion.37, bf16[3,768,768]{2,1,0:T(8,128)(2,1)} %param.14, s32[768]{0:T(1024)} %add_select_fusion, f32[64,768]{1,0:T(8,128)S(1)} %copy-done.4), kind=kOutput, calls=%fused_computation.13 | convolution fusion | flops 104466432 | bytes 1773568 | tf_op jit(solution)/shard_map/dot_general | solution.py:79
  115.9 4.1 %collective-permute-done.3 = f32[64,768]{1,0:T(8,128)} collective-permute-done((f32[64,768]{1,0:T(8,128)S(1)}, f32[64,768]{1,0:T(8,128)}, u32[]{:S(2)}, u32[]{:S(2)}) %collective-permute-start.3) | collective-permute-done | bytes 196640 | tf_op jit(solution)/shard_map/ppermute | solution.py:22
  120.0 2.4 fusion.15
  122.5 2.1 fusion.34
  124.6 31.4 %all-reduce.10.cloned.1.call-done = f32[64,768]{1,0:T(8,128)} async-done(((f32[64,768]{1,0:T(8,128)}), f32[64,768]{1,0:T(8,128)}) %all-reduce.10.cloned.1.call-update) | async-done | bytes 196624 | tf_op jit(solution)/shard_map/psum | solution.py:38
  156.0 2.1 fusion.35
  159.8 4.2 %collective-permute-done.4 = f32[64,768]{1,0:T(8,128)S(1)} collective-permute-done((f32[64,768]{1,0:T(8,128)S(1)}, f32[64,768]{1,0:T(8,128)S(1)}, u32[]{:S(2)}, u32[]{:S(2)}) %collective-permute-start.4) | collective-permute-done | bytes 196640 | tf_op jit(solution)/shard_map/ppermute | solution.py:15
  164.0 2.5 %collective-permute-start.5 = (f32[64,768]{1,0:T(8,128)S(1)}, f32[64,768]{1,0:T(8,128)S(1)}, u32[]{:S(2)}, u32[]{:S(2)}) collective-permute-start(f32[64,768]{1,0:T(8,128)S(1)} %add.71), channel_id=1, source_target_pairs={{0,2},{1,3},{2,0},{3,1},{4,6},{5,7},{6,4},{7,5},{8,10},{9,11},{10,... | collective-permute-start | bytes 589832 | tf_op jit(solution)/shard_map/ppermute | solution.py:15
  166.4 6.9 %collective-permute-done.5 = f32[64,768]{1,0:T(8,128)S(1)} collective-permute-done((f32[64,768]{1,0:T(8,128)S(1)}, f32[64,768]{1,0:T(8,128)S(1)}, u32[]{:S(2)}, u32[]{:S(2)}) %collective-permute-start.5) | collective-permute-done | bytes 196640 | tf_op jit(solution)/shard_map/ppermute | solution.py:15
  174.1 24.0 %all-reduce.12.cloned.1.call-done = f32[64,768]{1,0:T(8,128)} async-done(((f32[64,768]{1,0:T(8,128)}), f32[64,768]{1,0:T(8,128)}) %all-reduce.12.cloned.1.call-update) | async-done | bytes 196624 | tf_op jit(solution)/shard_map/psum | solution.py:83
  198.1 2.2 fusion.62
  201.2 32.5 %all-reduce.14.cloned.1.call-done = f32[64,1536]{1,0:T(8,128)} async-done(((f32[64,1536]{1,0:T(8,128)}), f32[64,1536]{1,0:T(8,128)}) %all-reduce.14.cloned.1.call-update) | async-done | bytes 393232 | tf_op jit(solution)/shard_map/psum | solution.py:38
  (51 shorter events, 15.1 us)
Async XLA Ops:
  7.2 190.9 %copy-start = (bf16[768,1536]{1,0:T(8,128)(2,1)S(1)}, bf16[768,1536]{1,0:T(8,128)(2,1)}, u32[]{:S(2)}) copy-start(bf16[768,1536]{1,0:T(8,128)(2,1)} %param.11) | copy-start | bytes 7077892
  7.2 2.7 %copy-start.8 = (s32[3,6,24]{2,1,0:T(8,128)S(1)}, s32[3,6,24]{2,1,0:T(8,128)}, u32[]{:S(2)}) copy-start(s32[3,6,24]{2,1,0:T(8,128)} %param.13) | copy-start | bytes 5188
  7.2 38.5 %all-reduce.6.cloned.1.call-start = ((), (), s32[]{:S(2)}) async-start(), calls=%async_computation | async-start | bytes 393216 | tf_op jit(solution)/shard_map/psum | solution.py:38
  9.8 89.0 %all-reduce.8.cloned.1.call-start = ((), (), s32[]{:S(2)}) async-start(), calls=%async_computation.1 | async-start | bytes 393216 | tf_op jit(solution)/shard_map/psum | solution.py:38
  11.0 51.9 %copy-start.1 = (f32[1,3,64,768]{3,2,1,0:T(8,128)S(1)}, f32[1,3,64,768]{3,2,1,0:T(8,128)}, u32[]{:S(2)}) copy-start(f32[1,3,64,768]{3,2,1,0:T(8,128)} %param.8) | copy-start | bytes 1769476
  47.8 5.7 %collective-permute-start = (f32[64,768]{1,0:T(8,128)S(1)}, f32[64,768]{1,0:T(8,128)S(1)}, u32[]{:S(2)}, u32[]{:S(2)}) collective-permute-start(f32[64,768]{1,0:T(8,128)S(1)} %fusion.11), channel_id=1, source_target_pairs={{0,1},{1,0},{2,3},{3,2},{4,5},{5,4},{6,7},{7,6},{8,9},{9,8},{10,11... | collective-permute-start | bytes 589832 | tf_op jit(solution)/shard_map/ppermute | solution.py:22
  53.6 11.7 %copy-start.9 = (s32[3,6,24]{2,1,0:T(8,128)S(1)}, s32[3,6,24]{2,1,0:T(8,128)}, u32[]{:S(2)}) copy-start(s32[3,6,24]{2,1,0:T(8,128)} %param.15) | copy-start | bytes 5188
  53.6 9.4 %collective-permute-start.1 = (f32[64,768]{1,0:T(8,128)S(1)}, f32[64,768]{1,0:T(8,128)S(1)}, u32[]{:S(2)}, u32[]{:S(2)}) collective-permute-start(f32[64,768]{1,0:T(8,128)S(1)} %add.64), channel_id=1, source_target_pairs={{0,2},{1,3},{2,0},{3,1},{4,6},{5,7},{6,4},{7,5},{8,10},{9,11},{10,... | collective-permute-start | bytes 589832 | tf_op jit(solution)/shard_map/ppermute | solution.py:22
  57.7 41.1 %copy-start.10 = (s32[768]{0:T(1024)S(1)}, s32[768]{0:T(1024)}, u32[]{:S(2)}) copy-start(s32[768]{0:T(1024)} %add_select_fusion) | copy-start | bytes 9220
  65.2 36.4 %copy-start.3 = (f32[64,768]{1,0:T(8,128)S(1)}, f32[64,768]{1,0:T(8,128)}, u32[]{:S(2)}) copy-start(f32[64,768]{1,0:T(8,128)} %all-reduce.6.cloned.1.call-done) | copy-start | bytes 589828
  65.2 90.8 %all-reduce.10.cloned.1.call-start = ((), (), s32[]{:S(2)}) async-start(), calls=%async_computation.2 | async-start | bytes 393216 | tf_op jit(solution)/shard_map/psum | solution.py:38
  101.7 11.4 %copy-start.4 = (f32[64,768]{1,0:T(8,128)S(1)}, f32[64,768]{1,0:T(8,128)}, u32[]{:S(2)}) copy-start(f32[64,768]{1,0:T(8,128)} %all-reduce.8.cloned.1.call-done) | copy-start | bytes 589828
  103.9 2.5 %copy-start.7 = (f32[64,768]{1,0:T(8,128)}, f32[64,768]{1,0:T(8,128)S(1)}, u32[]{:S(2)}) copy-start(f32[64,768]{1,0:T(8,128)S(1)} %fusion.33) | copy-start | bytes 589828
  103.9 5.7 %collective-permute-start.2 = (f32[64,768]{1,0:T(8,128)S(1)}, f32[64,768]{1,0:T(8,128)S(1)}, u32[]{:S(2)}, u32[]{:S(2)}) collective-permute-start(f32[64,768]{1,0:T(8,128)S(1)} %fusion.33), channel_id=1, source_target_pairs={{0,1},{1,0},{2,3},{3,2},{4,5},{5,4},{6,7},{7,6},{8,9},{9,8},{10,11... | collective-permute-start | bytes 589832 | tf_op jit(solution)/shard_map/ppermute | solution.py:22
  110.6 9.5 %collective-permute-start.3 = (f32[64,768]{1,0:T(8,128)S(1)}, f32[64,768]{1,0:T(8,128)}, u32[]{:S(2)}, u32[]{:S(2)}) collective-permute-start(f32[64,768]{1,0:T(8,128)S(1)} %add.67), channel_id=1, source_target_pairs={{0,2},{1,3},{2,0},{3,1},{4,6},{5,7},{6,4},{7,5},{8,10},{9,11},{10,... | collective-permute-start | bytes 589832 | tf_op jit(solution)/shard_map/ppermute | solution.py:22
  115.9 6.6 %copy-start.11 = (s32[768]{0:T(1024)S(1)}, s32[768]{0:T(1024)}, u32[]{:S(2)}) copy-start(s32[768]{0:T(1024)} %add_select_fusion) | copy-start | bytes 9220
  122.4 33.6 %copy-start.6 = (bf16[768,24]{1,0:T(8,128)(2,1)S(1)}, bf16[768,24]{1,0:T(8,128)(2,1)}, u32[]{:S(2)}) copy-start(bf16[768,24]{1,0:T(8,128)(2,1)} %fusion.36) | copy-start | bytes 110596
  122.4 75.6 %all-reduce.12.cloned.1.call-start = ((), (), s32[]{:S(2)}) async-start(), calls=%async_computation.3 | async-start | bytes 393216 | tf_op jit(solution)/shard_map/psum | solution.py:83
  158.2 39.9 %copy-start.2 = (f32[64,768]{1,0:T(8,128)S(1)}, f32[64,768]{1,0:T(8,128)}, u32[]{:S(2)}) copy-start(f32[64,768]{1,0:T(8,128)} %param.9) | copy-start | bytes 589828
  158.2 5.7 %collective-permute-start.4 = (f32[64,768]{1,0:T(8,128)S(1)}, f32[64,768]{1,0:T(8,128)S(1)}, u32[]{:S(2)}, u32[]{:S(2)}) collective-permute-start(f32[64,768]{1,0:T(8,128)S(1)} %fusion.35), channel_id=1, source_target_pairs={{0,1},{1,0},{2,3},{3,2},{4,5},{5,4},{6,7},{7,6},{8,9},{9,8},{10,11... | collective-permute-start | bytes 589832 | tf_op jit(solution)/shard_map/ppermute | solution.py:15
  164.0 9.3 %collective-permute-start.5 = (f32[64,768]{1,0:T(8,128)S(1)}, f32[64,768]{1,0:T(8,128)S(1)}, u32[]{:S(2)}, u32[]{:S(2)}) collective-permute-start(f32[64,768]{1,0:T(8,128)S(1)} %add.71), channel_id=1, source_target_pairs={{0,2},{1,3},{2,0},{3,1},{4,6},{5,7},{6,4},{7,5},{8,10},{9,11},{10,... | collective-permute-start | bytes 589832 | tf_op jit(solution)/shard_map/ppermute | solution.py:15
  174.0 26.2 %copy-start.5 = (f32[64,768]{1,0:T(8,128)S(1)}, f32[64,768]{1,0:T(8,128)}, u32[]{:S(2)}) copy-start(f32[64,768]{1,0:T(8,128)} %all-reduce.10.cloned.1.call-done) | copy-start | bytes 589828
  174.1 59.6 %all-reduce.14.cloned.1.call-start = ((), (), s32[]{:S(2)}) async-start(), calls=%async_computation.4 | async-start | bytes 786432 | tf_op jit(solution)/shard_map/psum | solution.py:38
Sparse Core Ops, SparseCore 0:
  10.9 34.7 all-reduce.5
  65.3 33.4 all-reduce.7
  122.6 33.4 all-reduce.9
  174.2 23.8 all-reduce.11
  200.8 32.7 all-reduce.13
